TPU v7x, 32 devices: a whole 2x2x4 slice. The times are simulated.
32 devices in a mesh: row: 2 (over y), col: 8 (over z, x), layer: 2 (over core).
Axes of the slice: x: 2, y: 2, z: 4, core: 2. Of those that a mesh axis runs over, the one named last changes fastest.
Arguments:
- anomaly_x: bfloat16 [8, 4096, 4096], P(None, 'row', ('layer', 'col')), may hold values from -0.09375 to 0.09375
- anomaly_y: bfloat16 [8, 4096, 4096], P(None, 'col', ('layer', 'row')), may hold values from -6 to 6
Outputs:
- covariance: bfloat16 [8, 4096, 4096], P('layer', 'row', 'col')
All inputs are finite; a program needn't handle non-finite values.
Results may differ from a plain program's by a relative error of at most 0.001.
Values may be sent and summed in bfloat16 or wider, within the bound.
No kernel may reach another device: no remote copies, remote signals or barrier semaphores. Data moves between devices by JAX's collectives and lax.ppermute only.
A program may use at most 192 MiB of HBM per device.

v0:
```python
import jax
import jax.numpy as jnp
from jax import lax
from jax.sharding import PartitionSpec as P


def on_device(anomaly_x, anomaly_y):
    panel_x = lax.all_gather(anomaly_x, "col", axis=2, tiled=True)
    partial_tile = jnp.einsum(
        "bik,bjk->bij",
        panel_x,
        lax.all_gather(anomaly_y, "row", axis=2, tiled=True),
        preferred_element_type=jnp.float32,
    )
    summed = lax.psum_scatter(partial_tile, "layer", scatter_dimension=0, tiled=True)
    return summed.astype(jnp.bfloat16)


def solution(mesh):
    placed = (P(None, "row", ("layer", "col")), P(None, "col", ("layer", "row")))
    return jax.shard_map(
        on_device, mesh=mesh, in_specs=placed, out_specs=P("layer", "row", "col"), check_vma=False
    )
```

profile of v0, /device:TPU:0, one launch (start us, length us, event | category | flops | bytes accessed | tf_op | source)
XLA Modules:
  0.0 1587.2 jit_solution(16807389690178058107)
XLA Ops:
  6.5 0.0 all-gather.5.cloned.1.call-start
  6.5 0.7 all-gather.5.cloned.1.call-update
  7.3 0.0 all-gather.3.cloned.1.call-start
  7.3 0.7 all-gather.3.cloned.1.call-update
  8.0 0.0 reduce-scatter.2.cloned.1.call-start
  8.1 202.4 %all-gather.5.cloned.1.call-done = bf16[8,512,2048]{2,1,0:T(8,128)(2,1)} async-done(((bf16[8,512,1024]{2,1,0:T(8,128)(2,1)}), bf16[8,512,2048]{2,1,0:T(8,128)(2,1)}) %all-gather.5.cloned.1.call-update) | async-done | bytes 16777232 | tf_op jit(solution)/shard_map/all_gather | solution.py:12
  210.5 1269.6 %all-gather.3.cloned.1.call-done = bf16[8,2048,2048]{2,1,0:T(8,128)(2,1)} async-done(((bf16[8,2048,256]{2,1,0:T(8,128)(2,1)}), bf16[8,2048,2048]{2,1,0:T(8,128)(2,1)}) %all-gather.3.cloned.1.call-update) | async-done | bytes 67108880 | tf_op jit(solution)/shard_map/all_gather | solution.py:8
  1480.0 49.1 %fusion = f32[8,2048,512]{2,1,0:T(8,128)} fusion(bf16[8,2048,2048]{2,1,0:T(8,128)(2,1)} %all-gather.3.cloned.1.call-done, bf16[8,512,2048]{2,1,0:T(8,128)(2,1)} %all-gather.5.cloned.1.call-done), kind=kOutput, calls=%fused_computation | convolution fusion | flops 34359738368 | bytes 117440512 | tf_op jit(solution)/shard_map/bik,bjk->bij/dot_general | solution.py:9
  1529.1 0.0 reduce-scatter.2.cloned.1.call-update
  1529.2 42.6 %reduce-scatter.2.cloned.1.call-done = f32[4,2048,512]{2,1,0:T(8,128)} async-done(((f32[8,2048,512]{2,1,0:T(8,128)}), f32[4,2048,512]{2,1,0:T(8,128)}) %reduce-scatter.2.cloned.1.call-update) | async-done | bytes 16777232 | tf_op jit(solution)/shard_map/reduce_scatter | solution.py:15
  1571.7 9.0 convert_element_type.3
Async XLA Ops:
  6.5 203.9 %all-gather.5.cloned.1.call-start = ((), (), s32[]{:S(2)}) async-start(), calls=%async_computation.2 | async-start | bytes 25165824 | tf_op jit(solution)/shard_map/all_gather | solution.py:12
  7.3 1472.8 %all-gather.3.cloned.1.call-start = ((), (), s32[]{:S(2)}) async-start(), calls=%async_computation.1 | async-start | bytes 75497472 | tf_op jit(solution)/shard_map/all_gather | solution.py:8
  8.0 1563.7 %reduce-scatter.2.cloned.1.call-start = ((), (), s32[]{:S(2)}) async-start(), calls=%async_computation.3 | async-start | bytes 50331648 | tf_op jit(solution)/shard_map/reduce_scatter | solution.py:15
Sparse Core Ops, SparseCore 0:
  8.9 201.5 all-gather.4
  211.9 1268.0 all-gather.2
  1529.3 42.4 reduce-scatter.1
where the time goes:
time: 1590 us
  waiting for transfers between devices  1520 us (96%)
  matrix products  49.1 us (3%)
    all_gather x1, waiting for transfers between devices, on_device(): panel_x = lax.all_gather(anomaly_x, 'col', axis=2, tiled=True)  1270 us
    all_gather x1, waiting for transfers between devices, on_device(): lax.all_gather(anomaly_y, 'row', axis=2, tiled=True)  202 us
    dot_general x1, matrix products, on_device(): jnp.einsum('bik,bjk->bij', panel_x, lax.all_gather(anomaly_y, 'row', axis...  49.1 us
    reduce_scatter x1, waiting for transfers between devices, on_device(): lax.psum_scatter(partial_tile, 'layer', scatter_dimension=0, tiled=True)  42.6 us
  transfers between devices with their start and end apart: 3, of which 3 were waited for; matrix products, arithmetic and copies ran while one was open for 0% of the time, Pallas kernels for 0%

commit v1 on v0

v1 whole, which is shorter than its diff:
```python
import jax
import jax.numpy as jnp
from jax import lax
from jax.experimental import pallas as pl
from jax.experimental.pallas import tpu as pltpu
from jax.sharding import Mesh, PartitionSpec as P


def gathered(anomaly_x, anomaly_y):
    panel_x = lax.all_gather(anomaly_x, "col", axis=2, tiled=True)
    partial_tile = jnp.einsum(
        "bik,bjk->bij",
        panel_x,
        lax.all_gather(anomaly_y, "row", axis=2, tiled=True),
        preferred_element_type=jnp.float32,
    )
    summed = lax.psum_scatter(partial_tile, "layer", scatter_dimension=0, tiled=True)
    return summed.astype(jnp.bfloat16)


def tile_kernel(upper_ref, *refs):
    xs, ys, out_ref = refs[:4], refs[4:8], refs[8]
    upper = upper_ref[0]
    nlayer, _, nx = xs[0].shape[:3]
    left, right = [], []
    for l in range(nlayer):
        for x_ref, (r, h) in zip(xs, ((0, 0), (0, 1), (1, 0), (1, 1))):
            for xx in range(nx):
                left.append(x_ref[l, 0, xx])
                right.append(ys[h * nx + xx][l, r ^ upper, 0])
    c = lax.dot_general(
        jnp.concatenate(left, 1),
        jnp.concatenate(right, 1),
        (((1,), (1,)), ((), ())),
        preferred_element_type=jnp.float32,
    )
    out_ref[0] = c.astype(out_ref.dtype)


def tiles(upper, outer, own, across, beyond, own_row, part, ys, dims):
    nrow, nx, nlayer = dims
    cols, kx = ys[0].shape[1:]
    shape5 = lambda a: a.reshape(nlayer, nrow, nx, *a.shape[1:])
    x_spec = lambda at: pl.BlockSpec((nlayer, 1, nx, part, kx), lambda j, i, u: (0, i, 0, at, 0))
    y_spec = pl.BlockSpec((nlayer, nrow, 1, cols, kx), lambda j, i, u: (0, 0, j, 0, 0))
    at = own_row // part
    depth = nlayer * 4 * nx * kx
    return pl.pallas_call(
        tile_kernel,
        grid_spec=pltpu.PrefetchScalarGridSpec(
            num_scalar_prefetch=1,
            grid=(nx, nrow),
            in_specs=[x_spec(0), x_spec(at), x_spec(at), x_spec(0)] + [y_spec] * 4,
            out_specs=pl.BlockSpec((1, part, cols), lambda j, i, u: (i * nx + j, 0, 0)),
        ),
        out_shape=jax.ShapeDtypeStruct((nrow * nx, part, cols), jnp.bfloat16),
        compiler_params=pltpu.CompilerParams(vmem_limit_bytes=48 << 20),
        cost_estimate=pl.CostEstimate(
            flops=2 * nrow * nx * part * cols * depth,
            bytes_accessed=2 * nx * depth * (nrow * part + cols),
            transcendentals=0,
        ),
    )(upper, *(shape5(a) for a in (outer, own, across, beyond)), *(shape5(a) for a in ys))


def pieces_of(blocks, cols):
    whole = [(c, 0, cols) for c in range(blocks - 1)]
    return whole + [(blocks - 1, 0, cols // 2), (blocks - 1, cols // 2, cols // 4), (blocks - 1, 3 * cols // 4, cols // 4)]


def line(sizes, x, y):
    nrow, nz, nx, nlayer = (sizes[a] for a in ("row", "z", "x", "layer"))
    _, rows, kx = x.shape
    _, cols, ky = y.shape
    z = lax.axis_index("z")
    inner = (z > 0) & (z < nz - 1)
    upper = z >= nz // 2
    inward = [(0, 1), (nz - 1, nz - 2)]
    outward = [(b, a) for a, b in inward]
    middle = [(nz // 2 - 1, nz // 2), (nz // 2, nz // 2 - 1)]
    blocks = ky // kx
    dims = (nrow, nx, nlayer)

    def permute(a, pairs):
        return lax.ppermute(a, "z", pairs)

    def spread(a):
        return lax.all_to_all(a, ("layer", "row", "x"), 0, 0, tiled=True)

    def x_block(c):
        return x[:, c * cols : (c + 1) * cols]

    def y_block(c):
        d = (c + blocks // 2) % blocks
        return jnp.where(upper, y[:, :, d * kx : (d + 1) * kx], y[:, :, c * kx : (c + 1) * kx])

    w, v, o1, m1 = [None] * blocks, [None] * blocks, [None] * blocks, [None] * blocks
    for c in range(blocks):
        w[c] = spread(jnp.where(inner, x_block(c), y_block(c)))
        o1[c] = permute(w[c], inward)
        m1[c] = permute(w[c], middle)
        v[c] = spread(jnp.where(inner, y_block(c), x_block(c)))
    flag = upper.astype(jnp.int32).reshape(1)
    out = jnp.zeros((nrow * nx, rows, cols), jnp.bfloat16)
    for c, first, part in pieces_of(blocks, cols):
        o2 = permute(v[c][:, first : first + part], inward)
        m2 = permute(o2, middle)
        far = tiles(flag, o2, w[c], m1[c], m2, first, part, o1, dims)
        near = tiles(flag, o2, w[c], m1[c], m2, first, part, v, dims)
        tile = jnp.where(inner, near, permute(far, outward))
        done = lax.all_to_all(tile, ("row", "x"), 0, 0, tiled=True)
        out = lax.dynamic_update_slice(out, done, (0, c * cols + first, 0))
    return out


def line_sizes(mesh):
    coords = [getattr(d, "coords", None) for d in mesh.devices[0, :, 0]]
    if any(c is None for c in coords):
        return None
    nx = len({c[0] for c in coords})
    return {
        "row": mesh.shape["row"],
        "z": mesh.shape["col"] // nx,
        "x": nx,
        "layer": mesh.shape["layer"],
    }


def fits(sizes, batch):
    return (
        sizes is not None
        and sizes["row"] * sizes["x"] * sizes["layer"] == batch
        and sizes["z"] == 2 * sizes["row"] == 2 * sizes["x"] == 4
    )


def solution(mesh):
    sizes = line_sizes(mesh)
    names = ("row", "z", "x", "layer")

    def plain(anomaly_x, anomaly_y):
        placed = (P(None, "row", ("layer", "col")), P(None, "col", ("layer", "row")))
        return jax.shard_map(
            gathered, mesh=mesh, in_specs=placed, out_specs=P("layer", "row", "col"), check_vma=False
        )(anomaly_x, anomaly_y)

    def body(x, y):
        return line(sizes, x, y)

    def lined(anomaly_x, anomaly_y):
        split = Mesh(mesh.devices.reshape([sizes[a] for a in names]), names)
        placed = (P(None, "row", ("layer", "z", "x")), P(None, ("z", "x"), ("layer", "row")))
        step = jax.shard_map(
            body, mesh=split, in_specs=placed, out_specs=P("layer", "row", ("z", "x")), check_vma=False
        )
        return step(anomaly_x, anomaly_y)

    def run(anomaly_x, anomaly_y):
        return (lined if fits(sizes, anomaly_x.shape[0]) else plain)(anomaly_x, anomaly_y)

    return run
```

time: 1590 us -> 747 us (0.47)
  waiting for transfers between devices: 1520 us -> 315 us
  Pallas kernels: 0 us -> 143 us
  blocking collectives: 0 us -> 121 us
  starting transfers between devices: 0.08 us -> 114 us
  matrix products: 49.1 us -> 0 us
  other arithmetic: 8.97 us -> 30.8 us
  local copies, waits for them, and re-layouts: 0 us -> 21.1 us
    all_gather x2 -> x0, waiting for transfers between devices: 1470 us -> none  [the longest x1 1270 us: on_device(): panel_x = lax.all_gather(anomaly_x, 'col', axis=2, tiled=True)]
    ppermute x0 -> x26, waiting for transfers between devices: none -> 286 us  [permute(): return lax.ppermute(a, 'z', pairs)]
    pallas_call x0 -> x12, Pallas kernels: none -> 143 us  [tiles(): pl.pallas_call(tile_kernel, grid_spec=pltpu.PrefetchScalarGridSpec(num_sc...]
    all_to_all x0 -> x4, blocking collectives: none -> 121 us  [spread(): return lax.all_to_all(a, ('layer', 'row', 'x'), 0, 0, tiled=True)]
    ppermute x0 -> x26, starting transfers between devices: none -> 70.8 us  [permute(): return lax.ppermute(a, 'z', pairs)]
    dot_general x1 -> x0, matrix products: 49.1 us -> none  [on_device(): jnp.einsum('bik,bjk->bij', panel_x, lax.all_gather(anomaly_y, 'row', axis...]
    all_to_all x0 -> x10, starting transfers between devices: none -> 43.2 us  [the longest x6 25.8 us: line(): done = lax.all_to_all(tile, ('row', 'x'), 0, 0, tiled=True)]
    reduce_scatter x1 -> x0, waiting for transfers between devices: 42.6 us -> none  [on_device(): lax.psum_scatter(partial_tile, 'layer', scatter_dimension=0, tiled=True)]
  transfers between devices with their start and end apart: 3 -> 36, of which waited for: 3 -> 15; matrix products, arithmetic and copies ran while one was open for 0% -> 6% of each run, Pallas kernels for 0% -> 19%
where the time goes in v1:
time: 747 us; the launch traced here: 745 us
  waiting for transfers between devices  315 us (42%)
  Pallas kernels  143 us (19%)
  blocking collectives  121 us (16%)
  starting transfers between devices  114 us (15%)
  other arithmetic  30.8 us (4%)
  local copies, waits for them, and re-layouts  21.1 us (3%)
    ppermute x26, waiting for transfers between devices, permute(): return lax.ppermute(a, 'z', pairs)  286 us
    pallas_call x12, Pallas kernels, tiles(): pl.pallas_call(tile_kernel, grid_spec=pltpu.PrefetchScalarGridSpec(num_sc...  143 us
    all_to_all x4, blocking collectives, spread(): return lax.all_to_all(a, ('layer', 'row', 'x'), 0, 0, tiled=True)  121 us
    ppermute x26, starting transfers between devices, permute(): return lax.ppermute(a, 'z', pairs)  70.8 us
    all_to_all x4, waiting for transfers between devices, spread(): return lax.all_to_all(a, ('layer', 'row', 'x'), 0, 0, tiled=True)  28.9 us
    all_to_all x6, starting transfers between devices, line(): done = lax.all_to_all(tile, ('row', 'x'), 0, 0, tiled=True)  25.8 us
    all_to_all x4, starting transfers between devices, spread(): return lax.all_to_all(a, ('layer', 'row', 'x'), 0, 0, tiled=True)  17.4 us
    select_n x2, other arithmetic, line(): w[c] = spread(jnp.where(inner, x_block(c), y_block(c)))  17.3 us
  transfers between devices with their start and end apart: 36, of which 15 were waited for; matrix products, arithmetic and copies ran while one was open for 6% of the time, Pallas kernels for 19%

profile of v1, /device:TPU:0, one launch (start us, length us, event | category | flops | bytes accessed | tf_op | source)
XLA Modules:
  0.0 745.0 jit_solution(6598260045352793492)
XLA Ops:
  0.0 9.0 %broadcast_select_fusion.4 = (bf16[8,512,256]{2,1,0:T(8,128)(2,1)S(1)}, bf16[8,512,256]{2,1,0:T(8,128)(2,1)S(1)}, bf16[8,512,256]{2,1,0:T(8,128)(2,1)}, bf16[8,512,256]{2,1,0:T(8,128)(2,1)}, bf16[8,512,256]{2,1,0:T(8,128)(2,1)}) fusion(pred[]{:T(512)S(6)} %and.4, bf16[8,2048,256]{2,1,0:T(8,128)(2,1)} %param.2, bf16[8,512,1024]{2,1,0:T(8,128)(2,1)} %param.3, ...), kind=kLoop, calls=%fused_computation.4 | loop fusion | flops 9437184 | bytes 27262978 | tf_op jit(solution)/shard_map/jit(_where)/select_n | solution.py:99
  9.0 31.2 %all_to_all.70 = bf16[8,512,256]{2,1,0:T(8,128)(2,1)S(1)} all-to-all(bf16[8,512,256]{2,1,0:T(8,128)(2,1)S(1)} %get-tuple-element.5), channel_id=1, replica_groups=mesh['row'=2,'z'=4,'x'=2,'layer'=2] {'layer','row','x'}, dimensions={0} | all-to-all | bytes 4194304 | tf_op jit(solution)/shard_map/all_to_all | solution.py:88
  40.2 29.4 %all_to_all.71 = bf16[8,512,256]{2,1,0:T(8,128)(2,1)} all-to-all(bf16[8,512,256]{2,1,0:T(8,128)(2,1)S(1)} %get-tuple-element.6), channel_id=1, replica_groups=mesh['row'=2,'z'=4,'x'=2,'layer'=2] {'layer','row','x'}, dimensions={0} | all-to-all | bytes 4194304 | tf_op jit(solution)/shard_map/all_to_all | solution.py:88
  73.9 8.4 %broadcast_select_fusion.5 = (bf16[8,512,256]{2,1,0:T(8,128)(2,1)}, bf16[8,512,256]{2,1,0:T(8,128)(2,1)}, bf16[8,512,256]{2,1,0:T(8,128)(2,1)}) fusion(pred[]{:T(512)S(6)} %and.4, bf16[8,2048,256]{2,1,0:T(8,128)(2,1)} %param.2, bf16[8,512,1024]{2,1,0:T(8,128)(2,1)} %param.3, pred[]{:T(512)S(6)} %ge.3), kind=kLoop, calls=%fused_computation.5 | loop fusion | flops 6291456 | bytes 20971522 | tf_op jit(solution)/shard_map/jit(_where)/select_n | solution.py:99
  82.3 17.7 %all-to-all-done.4 = bf16[8,512,256]{2,1,0:T(8,128)(2,1)} async-done(((bf16[8,512,256]{2,1,0:T(8,128)(2,1)}), bf16[8,512,256]{2,1,0:T(8,128)(2,1)}, u32[]{:S(2)}, u32[]{:S(2)}) %all-to-all-start.4) | async-done | bytes 2097184 | tf_op jit(solution)/shard_map/all_to_all | solution.py:88
  99.9 30.7 %all_to_all.72 = bf16[8,512,256]{2,1,0:T(8,128)(2,1)} all-to-all(bf16[8,512,256]{2,1,0:T(8,128)(2,1)} %get-tuple-element.11), channel_id=1, replica_groups=mesh['row'=2,'z'=4,'x'=2,'layer'=2] {'layer','row','x'}, dimensions={0} | all-to-all | bytes 4194304 | tf_op jit(solution)/shard_map/all_to_all | solution.py:88
  130.6 29.4 %all_to_all.73 = bf16[8,512,256]{2,1,0:T(8,128)(2,1)} all-to-all(bf16[8,512,256]{2,1,0:T(8,128)(2,1)S(1)} %copy-done), channel_id=1, replica_groups=mesh['row'=2,'z'=4,'x'=2,'layer'=2] {'layer','row','x'}, dimensions={0} | all-to-all | bytes 4194304 | tf_op jit(solution)/shard_map/all_to_all | solution.py:88
  179.2 11.3 %all-to-all-done.2 = bf16[8,512,256]{2,1,0:T(8,128)(2,1)} async-done(((bf16[8,512,256]{2,1,0:T(8,128)(2,1)}), bf16[8,512,256]{2,1,0:T(8,128)(2,1)}, u32[]{:S(2)}, u32[]{:S(2)}) %all-to-all-start.2) | async-done | bytes 2097184 | tf_op jit(solution)/shard_map/all_to_all | solution.py:88
  194.8 30.3 %collective-permute-done.20 = bf16[8,128,256]{2,1,0:T(8,128)(2,1)S(1)} collective-permute-done((bf16[8,128,256]{2,1,0:T(8,128)(2,1)S(1)}, bf16[8,128,256]{2,1,0:T(8,128)(2,1)S(1)}, u32[]{:S(2)}, u32[]{:S(2)}) %collective-permute-start.20) | collective-permute-done | bytes 524320 | tf_op jit(solution)/shard_map/ppermute | solution.py:85
  225.8 8.5 %collective-permute-start.3 = (bf16[8,512,256]{2,1,0:T(8,128)(2,1)}, bf16[8,512,256]{2,1,0:T(8,128)(2,1)}, u32[]{:S(2)}, u32[]{:S(2)}) collective-permute-start(bf16[8,512,256]{2,1,0:T(8,128)(2,1)} %all_to_all.71), channel_id=1, source_target_pairs={{0,4},{12,8},{1,5},{13,9},{2,6},{14,10},{3,7},{15,11},{16,20},{28,... | collective-permute-start | bytes 6291464 | tf_op jit(solution)/shard_map/ppermute | solution.py:85
  234.3 11.2 %collective-permute-start.8 = (bf16[8,512,256]{2,1,0:T(8,128)(2,1)}, bf16[8,512,256]{2,1,0:T(8,128)(2,1)}, u32[]{:S(2)}, u32[]{:S(2)}) collective-permute-start(bf16[8,512,256]{2,1,0:T(8,128)(2,1)} %all-to-all-done.2), channel_id=1, source_target_pairs={{0,4},{12,8},{1,5},{13,9},{2,6},{14,10},{3,7},{15,11},{16,20},{28,... | collective-permute-start | bytes 6291464 | tf_op jit(solution)/shard_map/ppermute | solution.py:85
  263.1 29.6 %collective-permute-done.3 = bf16[8,512,256]{2,1,0:T(8,128)(2,1)} collective-permute-done((bf16[8,512,256]{2,1,0:T(8,128)(2,1)}, bf16[8,512,256]{2,1,0:T(8,128)(2,1)}, u32[]{:S(2)}, u32[]{:S(2)}) %collective-permute-start.3) | collective-permute-done | bytes 2097184 | tf_op jit(solution)/shard_map/ppermute | solution.py:85
  294.7 42.9 %collective-permute-done.8 = bf16[8,512,256]{2,1,0:T(8,128)(2,1)} collective-permute-done((bf16[8,512,256]{2,1,0:T(8,128)(2,1)}, bf16[8,512,256]{2,1,0:T(8,128)(2,1)}, u32[]{:S(2)}, u32[]{:S(2)}) %collective-permute-start.8) | collective-permute-done | bytes 2097184 | tf_op jit(solution)/shard_map/ppermute | solution.py:85
  339.6 42.9 %collective-permute-done.4 = bf16[8,512,256]{2,1,0:T(8,128)(2,1)} collective-permute-done((bf16[8,512,256]{2,1,0:T(8,128)(2,1)}, bf16[8,512,256]{2,1,0:T(8,128)(2,1)}, u32[]{:S(2)}, u32[]{:S(2)}) %collective-permute-start.4) | collective-permute-done | bytes 2097184 | tf_op jit(solution)/shard_map/ppermute | solution.py:85
  384.2 43.3 %collective-permute-done.5 = bf16[8,512,256]{2,1,0:T(8,128)(2,1)} collective-permute-done((bf16[8,512,256]{2,1,0:T(8,128)(2,1)}, bf16[8,512,256]{2,1,0:T(8,128)(2,1)}, u32[]{:S(2)}, u32[]{:S(2)}) %collective-permute-start.5) | collective-permute-done | bytes 2097184 | tf_op jit(solution)/shard_map/ppermute | solution.py:85
  427.5 5.7 collective-permute-start.12
  433.2 9.1 %shard_map.37 = bf16[4,128,512]{2,1,0:T(8,128)(2,1)S(1)} custom-call(s32[1]{0:T(128)} %bitcast.upper_ref, bf16[2,2,2,128,256]{4,3,2,1,0:T(8,128)(2,1)S(1)} %bitcast.37, bf16[2,2,2,512,256]{4,3,2,1,0:T(8,128)(2,1)S(1)} %bitcast.29, bf16[2,2,2,512,256]{4,3,2,1,0:T(8,128)(2,1)} %bitcast.23.refs_2_, bf16[2,2,2,128,256]{4,3,2,1,0:T(8,128)(2,1)S(1)} %bitcast.39, ...), custom_call_target="tpu_custom_call" | custom-call | flops 2147483648 | bytes 12582912 | tf_op jit(solution)/shard_map/pallas_call | solution.py:48
  442.3 9.1 %shard_map.36 = bf16[4,128,512]{2,1,0:T(8,128)(2,1)S(1)} custom-call(s32[1]{0:T(128)} %bitcast.upper_ref, bf16[2,2,2,128,256]{4,3,2,1,0:T(8,128)(2,1)S(1)} %bitcast.38, bf16[2,2,2,512,256]{4,3,2,1,0:T(8,128)(2,1)S(1)} %bitcast.30, bf16[2,2,2,512,256]{4,3,2,1,0:T(8,128)(2,1)} %bitcast.23.refs_2_, bf16[2,2,2,128,256]{4,3,2,1,0:T(8,128)(2,1)S(1)} %bitcast.40, ...), custom_call_target="tpu_custom_call" | custom-call | flops 2147483648 | bytes 12582912 | tf_op jit(solution)/shard_map/pallas_call | solution.py:48
  453.4 19.0 %collective-permute-done = bf16[8,512,256]{2,1,0:T(8,128)(2,1)} collective-permute-done((bf16[8,512,256]{2,1,0:T(8,128)(2,1)}, bf16[8,512,256]{2,1,0:T(8,128)(2,1)}, u32[]{:S(2)}, u32[]{:S(2)}) %collective-permute-start) | collective-permute-done | bytes 2097184 | tf_op jit(solution)/shard_map/ppermute | solution.py:85
  474.4 10.1 %shard_map.35 = bf16[4,256,512]{2,1,0:T(8,128)(2,1)} custom-call(s32[1]{0:T(128)} %bitcast.upper_ref, bf16[2,2,2,256,256]{4,3,2,1,0:T(8,128)(2,1)} %bitcast.21.refs_0_, bf16[2,2,2,512,256]{4,3,2,1,0:T(8,128)(2,1)S(1)} %bitcast.31, bf16[2,2,2,512,256]{4,3,2,1,0:T(8,128)(2,1)} %bitcast.23.refs_2_, bf16[2,2,2,256,256]{4,3,2,1,0:T(8,128)(2,1)} %bitcast.24.refs_3_, ...), custom_call_target="tpu_custom_call" | custom-call | flops 4294967296 | bytes 16777216 | tf_op jit(solution)/shard_map/pallas_call | solution.py:48
  484.5 9.3 %shard_map.34 = bf16[4,256,512]{2,1,0:T(8,128)(2,1)S(1)} custom-call(s32[1]{0:T(128)} %bitcast.upper_ref, bf16[2,2,2,256,256]{4,3,2,1,0:T(8,128)(2,1)} %bitcast.21.refs_0_, bf16[2,2,2,512,256]{4,3,2,1,0:T(8,128)(2,1)S(1)} %bitcast.32, bf16[2,2,2,512,256]{4,3,2,1,0:T(8,128)(2,1)} %bitcast.23.refs_2_, bf16[2,2,2,256,256]{4,3,2,1,0:T(8,128)(2,1)} %bitcast.24.refs_3_, ...), custom_call_target="tpu_custom_call" | custom-call | flops 4294967296 | bytes 16777216 | tf_op jit(solution)/shard_map/pallas_call | solution.py:48
  496.4 15.2 %shard_map.31 = bf16[4,512,512]{2,1,0:T(8,128)(2,1)} custom-call(s32[1]{0:T(128)} %bitcast.upper_ref, bf16[2,2,2,512,256]{4,3,2,1,0:T(8,128)(2,1)} %bitcast.13.refs_0_, bf16[2,2,2,512,256]{4,3,2,1,0:T(8,128)(2,1)} %bitcast.45, bf16[2,2,2,512,256]{4,3,2,1,0:T(8,128)(2,1)} %bitcast.15.refs_2_, bf16[2,2,2,512,256]{4,3,2,1,0:T(8,128)(2,1)} %bitcast.16.refs_3_, ...), custom_call_target="tpu_custom_call" | custom-call | flops 8589934592 | bytes 25165824 | tf_op jit(solution)/shard_map/pallas_call | solution.py:48
  520.2 14.2 %collective-permute-done.19 = bf16[4,256,512]{2,1,0:T(8,128)(2,1)} collective-permute-done((bf16[4,256,512]{2,1,0:T(8,128)(2,1)}, bf16[4,256,512]{2,1,0:T(8,128)(2,1)}, u32[]{:S(2)}, u32[]{:S(2)}) %collective-permute-start.19) | collective-permute-done | bytes 1048608 | tf_op jit(solution)/shard_map/ppermute | solution.py:85
  540.1 15.2 %shard_map.29 = bf16[4,512,512]{2,1,0:T(8,128)(2,1)} custom-call(s32[1]{0:T(128)} %bitcast.upper_ref, bf16[2,2,2,512,256]{4,3,2,1,0:T(8,128)(2,1)} %bitcast.1.refs_0_, bf16[2,2,2,512,256]{4,3,2,1,0:T(8,128)(2,1)} %bitcast.2.refs_1_, bf16[2,2,2,512,256]{4,3,2,1,0:T(8,128)(2,1)} %bitcast.3.refs_2_, bf16[2,2,2,512,256]{4,3,2,1,0:T(8,128)(2,1)} %bitcast.4.refs_3_, ...), custom_call_target="tpu_custom_call" | custom-call | flops 8589934592 | bytes 25165824 | tf_op jit(solution)/shard_map/pallas_call | solution.py:48
  561.0 14.0 %shard_map.30 = bf16[4,512,512]{2,1,0:T(8,128)(2,1)S(1)} custom-call(s32[1]{0:T(128)} %bitcast.upper_ref, bf16[2,2,2,512,256]{4,3,2,1,0:T(8,128)(2,1)} %bitcast.13.refs_0_, bf16[2,2,2,512,256]{4,3,2,1,0:T(8,128)(2,1)} %bitcast.46, bf16[2,2,2,512,256]{4,3,2,1,0:T(8,128)(2,1)} %bitcast.15.refs_2_, bf16[2,2,2,512,256]{4,3,2,1,0:T(8,128)(2,1)} %bitcast.16.refs_3_, ...), custom_call_target="tpu_custom_call" | custom-call | flops 8589934592 | bytes 25165824 | tf_op jit(solution)/shard_map/pallas_call | solution.py:48
  587.0 15.2 %shard_map.33 = bf16[4,512,512]{2,1,0:T(8,128)(2,1)} custom-call(s32[1]{0:T(128)} %bitcast.upper_ref, bf16[2,2,2,512,256]{4,3,2,1,0:T(8,128)(2,1)} %bitcast.17.refs_0_, bf16[2,2,2,512,256]{4,3,2,1,0:T(8,128)(2,1)} %bitcast.43, bf16[2,2,2,512,256]{4,3,2,1,0:T(8,128)(2,1)} %bitcast.19.refs_2_, bf16[2,2,2,512,256]{4,3,2,1,0:T(8,128)(2,1)} %bitcast.20.refs_3_, ...), custom_call_target="tpu_custom_call" | custom-call | flops 8589934592 | bytes 25165824 | tf_op jit(solution)/shard_map/pallas_call | solution.py:48
  603.5 14.0 %shard_map.28 = bf16[4,512,512]{2,1,0:T(8,128)(2,1)S(1)} custom-call(s32[1]{0:T(128)} %bitcast.upper_ref, bf16[2,2,2,512,256]{4,3,2,1,0:T(8,128)(2,1)} %bitcast.1.refs_0_, bf16[2,2,2,512,256]{4,3,2,1,0:T(8,128)(2,1)} %bitcast.2.refs_1_, bf16[2,2,2,512,256]{4,3,2,1,0:T(8,128)(2,1)} %bitcast.3.refs_2_, bf16[2,2,2,512,256]{4,3,2,1,0:T(8,128)(2,1)} %bitcast.4.refs_3_, ...), custom_call_target="tpu_custom_call" | custom-call | flops 8589934592 | bytes 25165824 | tf_op jit(solution)/shard_map/pallas_call | solution.py:48
  630.6 14.0 %shard_map.32 = bf16[4,512,512]{2,1,0:T(8,128)(2,1)S(1)} custom-call(s32[1]{0:T(128)} %bitcast.upper_ref, bf16[2,2,2,512,256]{4,3,2,1,0:T(8,128)(2,1)} %bitcast.17.refs_0_, bf16[2,2,2,512,256]{4,3,2,1,0:T(8,128)(2,1)} %bitcast.44, bf16[2,2,2,512,256]{4,3,2,1,0:T(8,128)(2,1)} %bitcast.19.refs_2_, bf16[2,2,2,512,256]{4,3,2,1,0:T(8,128)(2,1)} %bitcast.20.refs_3_, ...), custom_call_target="tpu_custom_call" | custom-call | flops 8589934592 | bytes 25165824 | tf_op jit(solution)/shard_map/pallas_call | solution.py:48
  644.6 49.0 %collective-permute-done.15 = bf16[4,512,512]{2,1,0:T(8,128)(2,1)} collective-permute-done((bf16[4,512,512]{2,1,0:T(8,128)(2,1)}, bf16[4,512,512]{2,1,0:T(8,128)(2,1)}, u32[]{:S(2)}, u32[]{:S(2)}) %collective-permute-start.15) | collective-permute-done | bytes 2097184 | tf_op jit(solution)/shard_map/ppermute | solution.py:85
  701.2 9.1 %shard_map.39 = bf16[4,128,512]{2,1,0:T(8,128)(2,1)S(1)} custom-call(s32[1]{0:T(128)} %bitcast.upper_ref, bf16[2,2,2,128,256]{4,3,2,1,0:T(8,128)(2,1)S(1)} %bitcast.35, bf16[2,2,2,512,256]{4,3,2,1,0:T(8,128)(2,1)S(1)} %bitcast.33, bf16[2,2,2,512,256]{4,3,2,1,0:T(8,128)(2,1)} %bitcast.23.refs_2_, bf16[2,2,2,128,256]{4,3,2,1,0:T(8,128)(2,1)S(1)} %bitcast.41, ...), custom_call_target="tpu_custom_call" | custom-call | flops 2147483648 | bytes 12582912 | tf_op jit(solution)/shard_map/pallas_call | solution.py:48
  711.7 9.1 %shard_map.38 = bf16[4,128,512]{2,1,0:T(8,128)(2,1)S(1)} custom-call(s32[1]{0:T(128)} %bitcast.upper_ref, bf16[2,2,2,128,256]{4,3,2,1,0:T(8,128)(2,1)S(1)} %bitcast.36, bf16[2,2,2,512,256]{4,3,2,1,0:T(8,128)(2,1)S(1)} %bitcast.34, bf16[2,2,2,512,256]{4,3,2,1,0:T(8,128)(2,1)} %bitcast.23.refs_2_, bf16[2,2,2,128,256]{4,3,2,1,0:T(8,128)(2,1)S(1)} %bitcast.42, ...), custom_call_target="tpu_custom_call" | custom-call | flops 2147483648 | bytes 12582912 | tf_op jit(solution)/shard_map/pallas_call | solution.py:48
  724.5 5.7 dynamic_update_slice.18
  (74 shorter events, 132.1 us)
Async XLA Ops:
  69.5 30.4 %all-to-all-start.4 = ((bf16[8,512,256]{2,1,0:T(8,128)(2,1)}), bf16[8,512,256]{2,1,0:T(8,128)(2,1)}, u32[]{:S(2)}, u32[]{:S(2)}) async-start(bf16[8,512,256]{2,1,0:T(8,128)(2,1)} %get-tuple-element.9), calls=%async_computation.4 | async-start | bytes 4194304 | tf_op jit(solution)/shard_map/all_to_all | solution.py:88
  160.0 30.4 %all-to-all-start.2 = ((bf16[8,512,256]{2,1,0:T(8,128)(2,1)}), bf16[8,512,256]{2,1,0:T(8,128)(2,1)}, u32[]{:S(2)}, u32[]{:S(2)}) async-start(bf16[8,512,256]{2,1,0:T(8,128)(2,1)} %get-tuple-element.7), calls=%async_computation.2 | async-start | bytes 4194304 | tf_op jit(solution)/shard_map/all_to_all | solution.py:88
  164.4 89.0 %collective-permute-start.6 = (bf16[8,512,256]{2,1,0:T(8,128)(2,1)S(1)}, bf16[8,512,256]{2,1,0:T(8,128)(2,1)}, u32[]{:S(2)}, u32[]{:S(2)}) collective-permute-start(bf16[8,512,256]{2,1,0:T(8,128)(2,1)S(1)} %all_to_all.70), channel_id=1, source_target_pairs={{0,4},{12,8},{1,5},{13,9},{2,6},{14,10},{3,7},{15,11},{16,20},{28,... | collective-permute-start | bytes 6291464 | tf_op jit(solution)/shard_map/ppermute | solution.py:85
  171.3 53.8 %collective-permute-start.20 = (bf16[8,128,256]{2,1,0:T(8,128)(2,1)S(1)}, bf16[8,128,256]{2,1,0:T(8,128)(2,1)S(1)}, u32[]{:S(2)}, u32[]{:S(2)}) collective-permute-start(bf16[8,128,256]{2,1,0:T(8,128)(2,1)S(1)} %get-tuple-element.14), channel_id=1, source_target_pairs={{0,4},{12,8},{1,5},{13,9},{2,6},{14,10},{3,7},{15,11},{16,20},{28,... | collective-permute-start | bytes 1572872 | tf_op jit(solution)/shard_map/ppermute | solution.py:85
  174.9 72.8 %collective-permute-start.16 = (bf16[8,256,256]{2,1,0:T(8,128)(2,1)}, bf16[8,256,256]{2,1,0:T(8,128)(2,1)}, u32[]{:S(2)}, u32[]{:S(2)}) collective-permute-start(bf16[8,256,256]{2,1,0:T(8,128)(2,1)} %slice.60), channel_id=1, source_target_pairs={{0,4},{12,8},{1,5},{13,9},{2,6},{14,10},{3,7},{15,11},{16,20},{28,... | collective-permute-start | bytes 3145736 | tf_op jit(solution)/shard_map/ppermute | solution.py:85
  177.1 83.2 %collective-permute-start.17 = (bf16[8,512,256]{2,1,0:T(8,128)(2,1)S(1)}, bf16[8,512,256]{2,1,0:T(8,128)(2,1)}, u32[]{:S(2)}, u32[]{:S(2)}) collective-permute-start(bf16[8,512,256]{2,1,0:T(8,128)(2,1)S(1)} %all_to_all.70), channel_id=1, source_target_pairs={{4,8},{8,4},{5,9},{9,5},{6,10},{10,6},{7,11},{11,7},{20,24},{24,20... | collective-permute-start | bytes 6291464 | tf_op jit(solution)/shard_map/ppermute | solution.py:85
  190.4 65.6 %all-to-all-start = ((bf16[8,512,256]{2,1,0:T(8,128)(2,1)}), bf16[8,512,256]{2,1,0:T(8,128)(2,1)}, u32[]{:S(2)}, u32[]{:S(2)}) async-start(bf16[8,512,256]{2,1,0:T(8,128)(2,1)} %get-tuple-element.12), calls=%async_computation | async-start | bytes 4194304 | tf_op jit(solution)/shard_map/all_to_all | solution.py:88
  225.8 66.8 %collective-permute-start.3 = (bf16[8,512,256]{2,1,0:T(8,128)(2,1)}, bf16[8,512,256]{2,1,0:T(8,128)(2,1)}, u32[]{:S(2)}, u32[]{:S(2)}) collective-permute-start(bf16[8,512,256]{2,1,0:T(8,128)(2,1)} %all_to_all.71), channel_id=1, source_target_pairs={{0,4},{12,8},{1,5},{13,9},{2,6},{14,10},{3,7},{15,11},{16,20},{28,... | collective-permute-start | bytes 6291464 | tf_op jit(solution)/shard_map/ppermute | solution.py:85
  234.3 103.3 %collective-permute-start.8 = (bf16[8,512,256]{2,1,0:T(8,128)(2,1)}, bf16[8,512,256]{2,1,0:T(8,128)(2,1)}, u32[]{:S(2)}, u32[]{:S(2)}) collective-permute-start(bf16[8,512,256]{2,1,0:T(8,128)(2,1)} %all-to-all-done.2), channel_id=1, source_target_pairs={{0,4},{12,8},{1,5},{13,9},{2,6},{14,10},{3,7},{15,11},{16,20},{28,... | collective-permute-start | bytes 6291464 | tf_op jit(solution)/shard_map/ppermute | solution.py:85
  247.7 134.8 %collective-permute-start.4 = (bf16[8,512,256]{2,1,0:T(8,128)(2,1)}, bf16[8,512,256]{2,1,0:T(8,128)(2,1)}, u32[]{:S(2)}, u32[]{:S(2)}) collective-permute-start(bf16[8,512,256]{2,1,0:T(8,128)(2,1)} %all_to_all.72), channel_id=1, source_target_pairs={{0,4},{12,8},{1,5},{13,9},{2,6},{14,10},{3,7},{15,11},{16,20},{28,... | collective-permute-start | bytes 6291464 | tf_op jit(solution)/shard_map/ppermute | solution.py:85
  253.4 174.1 %collective-permute-start.5 = (bf16[8,512,256]{2,1,0:T(8,128)(2,1)}, bf16[8,512,256]{2,1,0:T(8,128)(2,1)}, u32[]{:S(2)}, u32[]{:S(2)}) collective-permute-start(bf16[8,512,256]{2,1,0:T(8,128)(2,1)} %all_to_all.73), channel_id=1, source_target_pairs={{0,4},{12,8},{1,5},{13,9},{2,6},{14,10},{3,7},{15,11},{16,20},{28,... | collective-permute-start | bytes 6291464 | tf_op jit(solution)/shard_map/ppermute | solution.py:85
  256.0 128.2 %all-to-all-start.3 = ((bf16[8,512,256]{2,1,0:T(8,128)(2,1)}), bf16[8,512,256]{2,1,0:T(8,128)(2,1)}, u32[]{:S(2)}, u32[]{:S(2)}) async-start(bf16[8,512,256]{2,1,0:T(8,128)(2,1)} %get-tuple-element.8), calls=%async_computation.3 | async-start | bytes 4194304 | tf_op jit(solution)/shard_map/all_to_all | solution.py:88
  260.3 212.1 %collective-permute-start = (bf16[8,512,256]{2,1,0:T(8,128)(2,1)}, bf16[8,512,256]{2,1,0:T(8,128)(2,1)}, u32[]{:S(2)}, u32[]{:S(2)}) collective-permute-start(bf16[8,512,256]{2,1,0:T(8,128)(2,1)} %all-to-all-done), channel_id=1, source_target_pairs={{0,4},{12,8},{1,5},{13,9},{2,6},{14,10},{3,7},{15,11},{16,20},{28,... | collective-permute-start | bytes 6291464 | tf_op jit(solution)/shard_map/ppermute | solution.py:85
  292.6 201.2 %collective-permute-start.9 = (bf16[8,512,256]{2,1,0:T(8,128)(2,1)}, bf16[8,512,256]{2,1,0:T(8,128)(2,1)}, u32[]{:S(2)}, u32[]{:S(2)}) collective-permute-start(bf16[8,512,256]{2,1,0:T(8,128)(2,1)} %all_to_all.72), channel_id=1, source_target_pairs={{4,8},{8,4},{5,9},{9,5},{6,10},{10,6},{7,11},{11,7},{20,24},{24,20... | collective-permute-start | bytes 6291464 | tf_op jit(solution)/shard_map/ppermute | solution.py:85
  337.6 157.5 %collective-permute-start.10 = (bf16[8,512,256]{2,1,0:T(8,128)(2,1)}, bf16[8,512,256]{2,1,0:T(8,128)(2,1)}, u32[]{:S(2)}, u32[]{:S(2)}) collective-permute-start(bf16[8,512,256]{2,1,0:T(8,128)(2,1)} %collective-permute-done.8), channel_id=1, source_target_pairs={{4,8},{8,4},{5,9},{9,5},{6,10},{10,6},{7,11},{11,7},{20,24},{24,20... | collective-permute-start | bytes 6291464 | tf_op jit(solution)/shard_map/ppermute | solution.py:85
  382.5 68.9 %collective-permute-start.18 = (bf16[8,256,256]{2,1,0:T(8,128)(2,1)}, bf16[8,256,256]{2,1,0:T(8,128)(2,1)}, u32[]{:S(2)}, u32[]{:S(2)}) collective-permute-start(bf16[8,256,256]{2,1,0:T(8,128)(2,1)} %collective-permute-done.16), channel_id=1, source_target_pairs={{4,8},{8,4},{5,9},{9,5},{6,10},{10,6},{7,11},{11,7},{20,24},{24,20... | collective-permute-start | bytes 3145736 | tf_op jit(solution)/shard_map/ppermute | solution.py:85
  427.5 90.7 %collective-permute-start.12 = (bf16[8,512,256]{2,1,0:T(8,128)(2,1)}, bf16[8,512,256]{2,1,0:T(8,128)(2,1)}, u32[]{:S(2)}, u32[]{:S(2)}) collective-permute-start(bf16[8,512,256]{2,1,0:T(8,128)(2,1)} %all-to-all-done.3), channel_id=1, source_target_pairs={{0,4},{12,8},{1,5},{13,9},{2,6},{14,10},{3,7},{15,11},{16,20},{28,... | collective-permute-start | bytes 6291464 | tf_op jit(solution)/shard_map/ppermute | solution.py:85
  451.4 87.3 %collective-permute-start.1 = (bf16[8,512,256]{2,1,0:T(8,128)(2,1)}, bf16[8,512,256]{2,1,0:T(8,128)(2,1)}, u32[]{:S(2)}, u32[]{:S(2)}) collective-permute-start(bf16[8,512,256]{2,1,0:T(8,128)(2,1)} %all_to_all.71), channel_id=1, source_target_pairs={{4,8},{8,4},{5,9},{9,5},{6,10},{10,6},{7,11},{11,7},{20,24},{24,20... | collective-permute-start | bytes 6291464 | tf_op jit(solution)/shard_map/ppermute | solution.py:85
  472.4 67.6 %collective-permute-start.2 = (bf16[8,512,256]{2,1,0:T(8,128)(2,1)}, bf16[8,512,256]{2,1,0:T(8,128)(2,1)}, u32[]{:S(2)}, u32[]{:S(2)}) collective-permute-start(bf16[8,512,256]{2,1,0:T(8,128)(2,1)} %collective-permute-done), channel_id=1, source_target_pairs={{4,8},{8,4},{5,9},{9,5},{6,10},{10,6},{7,11},{11,7},{20,24},{24,20... | collective-permute-start | bytes 6291464 | tf_op jit(solution)/shard_map/ppermute | solution.py:85
  495.1 39.3 %collective-permute-start.19 = (bf16[4,256,512]{2,1,0:T(8,128)(2,1)}, bf16[4,256,512]{2,1,0:T(8,128)(2,1)}, u32[]{:S(2)}, u32[]{:S(2)}) collective-permute-start(bf16[4,256,512]{2,1,0:T(8,128)(2,1)} %shard_map.35), channel_id=1, source_target_pairs={{4,0},{8,12},{5,1},{9,13},{6,2},{10,14},{7,3},{11,15},{20,16},{24,... | collective-permute-start | bytes 3145736 | tf_op jit(solution)/shard_map/ppermute | solution.py:85
  511.9 67.5 %collective-permute-start.11 = (bf16[4,512,512]{2,1,0:T(8,128)(2,1)}, bf16[4,512,512]{2,1,0:T(8,128)(2,1)}, u32[]{:S(2)}, u32[]{:S(2)}) collective-permute-start(bf16[4,512,512]{2,1,0:T(8,128)(2,1)} %shard_map.31), channel_id=1, source_target_pairs={{4,0},{8,12},{5,1},{9,13},{6,2},{10,14},{7,3},{11,15},{20,16},{24,... | collective-permute-start | bytes 6291464 | tf_op jit(solution)/shard_map/ppermute | solution.py:85
  514.0 42.5 %all-to-all-start.12 = ((bf16[4,128,512]{2,1,0:T(8,128)(2,1)}), bf16[4,128,512]{2,1,0:T(8,128)(2,1)}, u32[]{:S(2)}, u32[]{:S(2)}) async-start(bf16[4,128,512]{2,1,0:T(8,128)(2,1)} %broadcast_select_fusion.17), calls=%async_computation.12 | async-start | bytes 1048576 | tf_op jit(solution)/shard_map/all_to_all | solution.py:111
  518.2 68.8 %collective-permute-start.13 = (bf16[8,512,256]{2,1,0:T(8,128)(2,1)}, bf16[8,512,256]{2,1,0:T(8,128)(2,1)}, u32[]{:S(2)}, u32[]{:S(2)}) collective-permute-start(bf16[8,512,256]{2,1,0:T(8,128)(2,1)} %all_to_all.73), channel_id=1, source_target_pairs={{4,8},{8,4},{5,9},{9,5},{6,10},{10,6},{7,11},{11,7},{20,24},{24,20... | collective-permute-start | bytes 6291464 | tf_op jit(solution)/shard_map/ppermute | solution.py:85
  534.4 52.6 %collective-permute-start.14 = (bf16[8,512,256]{2,1,0:T(8,128)(2,1)}, bf16[8,512,256]{2,1,0:T(8,128)(2,1)}, u32[]{:S(2)}, u32[]{:S(2)}) collective-permute-start(bf16[8,512,256]{2,1,0:T(8,128)(2,1)} %collective-permute-done.12), channel_id=1, source_target_pairs={{4,8},{8,4},{5,9},{9,5},{6,10},{10,6},{7,11},{11,7},{20,24},{24,20... | collective-permute-start | bytes 6291464 | tf_op jit(solution)/shard_map/ppermute | solution.py:85
  538.7 91.2 %collective-permute-start.23 = (bf16[8,128,256]{2,1,0:T(8,128)(2,1)}, bf16[8,128,256]{2,1,0:T(8,128)(2,1)S(1)}, u32[]{:S(2)}, u32[]{:S(2)}) collective-permute-start(bf16[8,128,256]{2,1,0:T(8,128)(2,1)} %get-tuple-element.13), channel_id=1, source_target_pairs={{0,4},{12,8},{1,5},{13,9},{2,6},{14,10},{3,7},{15,11},{16,20},{28,... | collective-permute-start | bytes 1572872 | tf_op jit(solution)/shard_map/ppermute | solution.py:85
  555.2 67.1 %collective-permute-start.7 = (bf16[4,512,512]{2,1,0:T(8,128)(2,1)}, bf16[4,512,512]{2,1,0:T(8,128)(2,1)}, u32[]{:S(2)}, u32[]{:S(2)}) collective-permute-start(bf16[4,512,512]{2,1,0:T(8,128)(2,1)} %shard_map.29), channel_id=1, source_target_pairs={{4,0},{8,12},{5,1},{9,13},{6,2},{10,14},{7,3},{11,15},{20,16},{24,... | collective-permute-start | bytes 6291464 | tf_op jit(solution)/shard_map/ppermute | solution.py:85
  556.5 26.0 %all-to-all-start.11 = ((bf16[4,256,512]{2,1,0:T(8,128)(2,1)}), bf16[4,256,512]{2,1,0:T(8,128)(2,1)}, u32[]{:S(2)}, u32[]{:S(2)}) async-start(bf16[4,256,512]{2,1,0:T(8,128)(2,1)} %broadcast_select_fusion.15), calls=%async_computation.11 | async-start | bytes 2097152 | tf_op jit(solution)/shard_map/all_to_all | solution.py:111
  582.6 42.9 %all-to-all-start.9 = ((bf16[4,512,512]{2,1,0:T(8,128)(2,1)}), bf16[4,512,512]{2,1,0:T(8,128)(2,1)}, u32[]{:S(2)}, u32[]{:S(2)}) async-start(bf16[4,512,512]{2,1,0:T(8,128)(2,1)} %broadcast_select_fusion.13), calls=%async_computation.9 | async-start | bytes 4194304 | tf_op jit(solution)/shard_map/all_to_all | solution.py:111
  602.2 91.4 %collective-permute-start.15 = (bf16[4,512,512]{2,1,0:T(8,128)(2,1)}, bf16[4,512,512]{2,1,0:T(8,128)(2,1)}, u32[]{:S(2)}, u32[]{:S(2)}) collective-permute-start(bf16[4,512,512]{2,1,0:T(8,128)(2,1)} %shard_map.33), channel_id=1, source_target_pairs={{4,0},{8,12},{5,1},{9,13},{6,2},{10,14},{7,3},{11,15},{20,16},{24,... | collective-permute-start | bytes 6291464 | tf_op jit(solution)/shard_map/ppermute | solution.py:85
  625.4 71.3 %all-to-all-start.8 = ((bf16[4,512,512]{2,1,0:T(8,128)(2,1)}), bf16[4,512,512]{2,1,0:T(8,128)(2,1)}, u32[]{:S(2)}, u32[]{:S(2)}) async-start(bf16[4,512,512]{2,1,0:T(8,128)(2,1)} %broadcast_select_fusion.14), calls=%async_computation.8 | async-start | bytes 4194304 | tf_op jit(solution)/shard_map/all_to_all | solution.py:111
  629.9 71.3 %collective-permute-start.24 = (bf16[8,128,256]{2,1,0:T(8,128)(2,1)S(1)}, bf16[8,128,256]{2,1,0:T(8,128)(2,1)S(1)}, u32[]{:S(2)}, u32[]{:S(2)}) collective-permute-start(bf16[8,128,256]{2,1,0:T(8,128)(2,1)S(1)} %collective-permute-done.23), channel_id=1, source_target_pairs={{4,8},{8,4},{5,9},{9,5},{6,10},{10,6},{7,11},{11,7},{20,24},{24,20... | collective-permute-start | bytes 1572872 | tf_op jit(solution)/shard_map/ppermute | solution.py:85
  696.8 36.4 %all-to-all-start.10 = ((bf16[4,512,512]{2,1,0:T(8,128)(2,1)}), bf16[4,512,512]{2,1,0:T(8,128)(2,1)}, u32[]{:S(2)}, u32[]{:S(2)}) async-start(bf16[4,512,512]{2,1,0:T(8,128)(2,1)} %broadcast_select_fusion.12), calls=%async_computation.10 | async-start | bytes 4194304 | tf_op jit(solution)/shard_map/all_to_all | solution.py:111
  (5 other events, 82.2 us)
